TPU v7x, 32 devices: a whole 2x2x4 slice. The times are simulated.
32 devices in a mesh: blk: 16 (over z, y, core), head: 2 (over x).
Axes of the slice: x: 2, y: 2, z: 4, core: 2. Of those that a mesh axis runs over, the one named last changes fastest.
Arguments:
- queries: bfloat16 [4096, 1024], P('blk', 'head'), may hold values from -216 to 216
- keys: bfloat16 [4096, 1024], P('blk', 'head'), may hold values from -6 to 6
- values: bfloat16 [4096, 1024], P('blk', 'head'), may hold values from -6 to 6
- group_table: int32 [16, 2], P('blk'), may hold values from 0 to 31, as said below
- doc_ids: int32 [4096], replicated, may hold values from 0 to 15, never falling along the last dimension, each value on 1 to 2048 neighbouring positions
Outputs:
- attended: bfloat16 [4096, 1024], P('blk', 'head')
Inputs may be any that keep to these rules, and one draw needn't show every extreme that they name: group_table[d, 1] = 31 - group_table[d, 0]; the first column holds each of 0 to 15 once. `doc_ids`: document numbers never fall along positions; a document holds at most 2048 positions.
All inputs are finite; a program needn't handle non-finite values.
Results may differ from a plain program's by a relative error of at most 0.0049.
Values may be sent and summed in bfloat16 or wider, within the bound.
A program may use at most 192 MiB of HBM per device.

v0:
```python
import math
import jax
import jax.numpy as jnp
from jax import lax
from jax.sharding import PartitionSpec as P

HEAD_DIM = 128


def shards(queries, keys, values, group_table, doc_ids):
    tok_rows = queries.shape[0]
    group_rows = tok_rows // 2
    head_count = queries.shape[1] // HEAD_DIM
    score_scale = 1.0 / math.sqrt(HEAD_DIM)
    whole_table = lax.all_gather(group_table, "blk", axis=0, tiled=True)
    group_docs = doc_ids.reshape(doc_ids.shape[0] // group_rows, group_rows)
    within = jnp.arange(group_rows, dtype=jnp.int32)
    stored_groups = whole_table.reshape(-1)
    all_key_pos = (stored_groups[:, None] * group_rows + within[None, :]).reshape(-1)
    all_key_doc = group_docs[stored_groups].reshape(-1)
    local_groups = group_table.reshape(-1)
    query_pos = (local_groups[:, None] * group_rows + within[None, :]).reshape(-1)
    query_doc = group_docs[local_groups].reshape(-1)
    query_heads = queries.reshape(tok_rows, head_count, HEAD_DIM)

    def attend_shard(running_state, key_piece, value_piece, offset):
        piece_rows = key_piece.shape[0]
        key_pos = lax.dynamic_slice_in_dim(all_key_pos, offset, piece_rows, 0)
        key_doc = lax.dynamic_slice_in_dim(all_key_doc, offset, piece_rows, 0)
        visible = (query_doc[:, None] == key_doc[None, :]) & (
            key_pos[None, :] <= query_pos[:, None]
        )
        summed, running_max, weight_sum = running_state
        key_heads = key_piece.reshape(piece_rows, head_count, HEAD_DIM)
        value_heads = value_piece.reshape(piece_rows, head_count, HEAD_DIM)
        scores = (
            jnp.einsum("qhd,khd->hqk", query_heads, key_heads, preferred_element_type=jnp.float32)
            * score_scale
        )
        scores = jnp.where(visible[None], scores, -1e30)
        new_max = jnp.maximum(running_max, jnp.max(scores, axis=-1))
        weights = jnp.where(visible[None], jnp.exp(scores - new_max[..., None]), 0.0)
        factor = jnp.exp(running_max - new_max)
        weight_sum = weight_sum * factor + jnp.sum(weights, axis=-1)
        summed = summed * jnp.transpose(factor)[..., None] + jnp.einsum(
            "hqk,khd->qhd",
            weights.astype(jnp.bfloat16),
            value_heads,
            preferred_element_type=jnp.float32,
        )
        return (summed, new_max, weight_sum)

    initial = (
        jnp.zeros((tok_rows, head_count, HEAD_DIM), jnp.float32),
        jnp.full((head_count, tok_rows), -1e30, jnp.float32),
        jnp.zeros((head_count, tok_rows), jnp.float32),
    )
    key_piece = lax.all_gather(keys, "blk", axis=0, tiled=True)
    value_piece = lax.all_gather(values, "blk", axis=0, tiled=True)
    shard_count = key_piece.shape[0] // tok_rows
    key_shards = key_piece.reshape(shard_count, tok_rows, key_piece.shape[1])
    value_shards = value_piece.reshape(shard_count, tok_rows, value_piece.shape[1])
    shard_ids = jnp.arange(shard_count, dtype=jnp.int32)

    def step(state_now, item):
        key_one, value_one, shard_index = item
        start = shard_index * tok_rows
        return (attend_shard(state_now, key_one, value_one, start), None)

    final_state, unused = lax.scan(step, initial, (key_shards, value_shards, shard_ids))
    summed, running_max, weight_sum = final_state
    output = summed / jnp.transpose(weight_sum)[..., None]
    return output.reshape(tok_rows, head_count * HEAD_DIM).astype(jnp.bfloat16)


def solution(mesh):
    in_specs = (P("blk", "head"), P("blk", "head"), P("blk", "head"), P("blk", None), P())
    out_specs = P("blk", "head")
    return jax.shard_map(shards, mesh=mesh, in_specs=in_specs, out_specs=out_specs, check_vma=False)
```

profile of v0, /device:TPU:0, one launch (start us, length us, event | category | flops | bytes accessed | tf_op | source)
XLA Modules:
  0.0 186.2 jit_solution(14628548293793121357)
XLA Ops:
  6.5 0.7 all-gather.4.cloned.1.call-update
  7.3 0.7 all-gather.6.cloned.1.call-update
  8.0 23.3 %all-gather = s32[16,1,2]{2,1,0:T(1,128)S(1)} all-gather(s32[1,1,2]{2,1,0:T(1,128)} %bitcast.68), channel_id=1, replica_groups=mesh['blk'=16,'head'=2] {'blk'}, dimensions={0}, use_global_device_ids=true | all-gather | bytes 136 | tf_op jit(solution)/shard_map/all_gather | solution.py:15
  31.4 0.5 broadcast.150
  31.9 0.7 multiply_reduce_fusion
  32.8 0.6 gather_fusion.1
  33.3 0.7 fusion.14
  34.0 0.6 gather_fusion
  34.6 1.1 copy.23
  35.8 0.7 multiply_bitcast_fusion
  36.6 26.1 %all-gather.4.cloned.1.call-done = bf16[4096,512]{1,0:T(8,128)(2,1)} async-done(((bf16[256,512]{1,0:T(8,128)(2,1)}), bf16[4096,512]{1,0:T(8,128)(2,1)}) %all-gather.4.cloned.1.call-update) | async-done | bytes 4194320 | tf_op jit(solution)/shard_map/all_gather | solution.py:58
  62.7 51.1 %all-gather.6.cloned.1.call-done = bf16[4096,512]{1,0:T(8,128)(2,1)} async-done(((bf16[256,512]{1,0:T(8,128)(2,1)}), bf16[4096,512]{1,0:T(8,128)(2,1)}) %all-gather.6.cloned.1.call-update) | async-done | bytes 4194320 | tf_op jit(solution)/shard_map/all_gather | solution.py:59
  113.8 64.7 %while.15 = (s32[]{:T(128)}, f32[256,4,128]{0,2,1:T(8,128)S(1)}, f32[4,256]{1,0:T(4,128)S(1)}, f32[4,256]{1,0:T(4,128)S(1)}, s32[2,128]{1,0:T(2,128)S(1)}, /*ind...) while((s32[]{:T(128)}, f32[256,4,128]{0,2,1:T(8,128)S(1)}, ...), condition=%wide.region_3.4_spmd.clone, body=%wide.region_0.3_spmd.clone.sunk | while | flops 137173248 | bytes 7415023 | solution.py:70
  113.8 0.6 dynamic_slice.29
  115.4 1.1 constant_dynamic-slice_fusion.3
  116.6 0.4 fusion.33
  117.4 0.4 fusion.35
  117.8 0.6 dynamic_slice.29
  119.4 1.1 constant_dynamic-slice_fusion.3
  120.6 0.4 fusion.33
  121.4 0.4 fusion.35
  121.9 0.6 dynamic_slice.29
  123.5 1.1 constant_dynamic-slice_fusion.3
  125.4 0.4 fusion.35
  125.9 0.6 dynamic_slice.29
  127.5 1.1 constant_dynamic-slice_fusion.3
  129.5 0.4 fusion.35
  129.9 0.6 dynamic_slice.29
  131.5 1.1 constant_dynamic-slice_fusion.3
  133.5 0.4 fusion.35
  134.0 0.6 dynamic_slice.29
  135.6 1.1 constant_dynamic-slice_fusion.3
  137.6 0.4 fusion.35
  138.0 0.6 dynamic_slice.29
  139.6 1.1 constant_dynamic-slice_fusion.3
  141.6 0.4 fusion.35
  142.1 0.6 dynamic_slice.29
  143.7 1.1 constant_dynamic-slice_fusion.3
  145.7 0.4 fusion.35
  146.1 0.6 dynamic_slice.29
  147.7 1.1 constant_dynamic-slice_fusion.3
  149.7 0.4 fusion.35
  150.2 0.6 dynamic_slice.29
  151.8 1.1 constant_dynamic-slice_fusion.3
  153.7 0.4 fusion.35
  154.2 0.6 dynamic_slice.29
  155.8 1.1 constant_dynamic-slice_fusion.3
  157.8 0.4 fusion.35
  158.2 0.6 dynamic_slice.29
  159.8 1.1 constant_dynamic-slice_fusion.3
  161.8 0.4 fusion.35
  162.3 0.6 dynamic_slice.29
  163.9 1.1 constant_dynamic-slice_fusion.3
  165.9 0.4 fusion.35
  166.3 0.6 dynamic_slice.29
  167.9 1.1 constant_dynamic-slice_fusion.3
  169.9 0.4 fusion.35
  170.4 0.6 dynamic_slice.29
  172.0 1.1 constant_dynamic-slice_fusion.3
  174.0 0.4 fusion.35
  174.4 0.6 dynamic_slice.29
  176.0 1.1 constant_dynamic-slice_fusion.3
  178.0 0.4 fusion.35
  178.5 0.8 copy.30
  (190 shorter events, 19.6 us)
Async XLA Ops:
  6.5 26.2 %copy-start = (s32[4096]{0:T(1024)S(1)}, s32[4096]{0:T(1024)}, u32[]{:S(2)}) copy-start(s32[4096]{0:T(1024)} %param.11) | copy-start | bytes 49156
  6.5 56.1 %all-gather.4.cloned.1.call-start = ((), (), s32[]{:S(2)}) async-start(), calls=%async_computation | async-start | bytes 4456448 | tf_op jit(solution)/shard_map/all_gather | solution.py:58
  7.3 106.5 %all-gather.6.cloned.1.call-start = ((), (), s32[]{:S(2)}) async-start(), calls=%async_computation.1 | async-start | bytes 4456448 | tf_op jit(solution)/shard_map/all_gather | solution.py:59
Sparse Core Ops, SparseCore 0:
  9.5 53.1 all-gather.3
  64.8 48.8 all-gather.5
where the time goes:
time: 187 us; the launch traced here: 186 us
  waiting for transfers between devices  78.6 us (42%)
  local copies, waits for them, and re-layouts  37.4 us (20%)
  blocking collectives  23.3 us (12%)
  between operations  13.5 us (7%)
  matrix products  12.7 us (7%)
  loops' own time  11.4 us (6%)
  other arithmetic  9.23 us (5%)
    all_gather x1, waiting for transfers between devices, shards(): value_piece = lax.all_gather(values, 'blk', axis=0, tiled=True)  51.1 us
    dynamic_slice x64, local copies, waits for them, and re-layouts, shards(): lax.scan(step, initial, (key_shards, value_shards, shard_ids))  31 us
    all_gather x1, waiting for transfers between devices, shards(): key_piece = lax.all_gather(keys, 'blk', axis=0, tiled=True)  26.1 us
    all_gather x1, blocking collectives, shards(): whole_table = lax.all_gather(group_table, 'blk', axis=0, tiled=True)  23.3 us
    another operation x1, loops' own time, shards(): lax.scan(step, initial, (key_shards, value_shards, shard_ids))  11.4 us
    dot_general x16, matrix products, attend_shard(): jnp.einsum('hqk,khd->qhd', weights.astype(jnp.bfloat16), value_heads, pre...  6.68 us
    dot_general x16, matrix products, attend_shard(): jnp.einsum('qhd,khd->hqk', query_heads, key_heads, preferred_element_type...  6.02 us
  transfers between devices with their start and end apart: 2, of which 2 were waited for; matrix products, arithmetic and copies ran while one was open for 3% of the time, Pallas kernels for 0%

commit v1 on v0

--- a/solution.py
+++ b/solution.py
@@ -56,7 +56,13 @@
         jnp.zeros((head_count, tok_rows), jnp.float32),
     )
     key_piece = lax.all_gather(keys, "blk", axis=0, tiled=True)
-    value_piece = lax.all_gather(values, "blk", axis=0, tiled=True)
+    nd = lax.psum(1, "blk")
+    made = [values]
+    for b in range(nd - 1):
+        lower = lax.ppermute(made[-1], "blk", [(d, (d + 1) % nd) for d in range(nd)])
+        made.append(lower)
+    parts_out = jnp.concatenate(made[::-1], axis=0)
+    value_piece = jnp.roll(parts_out, (lax.axis_index("blk") + 1) * values.shape[0], axis=0)
     shard_count = key_piece.shape[0] // tok_rows
     key_shards = key_piece.reshape(shard_count, tok_rows, key_piece.shape[1])
     value_shards = value_piece.reshape(shard_count, tok_rows, value_piece.shape[1])

time: 187 us -> 245 us (1.31)
  waiting for transfers between devices: 78.6 us -> 126 us
  local copies, waits for them, and re-layouts: 37.4 us -> 50.3 us
  blocking collectives: 23.3 us -> 18.2 us
    ppermute x0 -> x15, waiting for transfers between devices: none -> 126 us  [shards(): lax.ppermute(made[-1], 'blk', [(d, (d + 1) % nd) for d in range(nd)])]
    all_gather x1 -> x0, waiting for transfers between devices: 51.1 us -> none  [shards(): value_piece = lax.all_gather(values, 'blk', axis=0, tiled=True)]
    all_gather x1, waiting for transfers between devices: 26.1 us -> 0.01 us  [shards(): key_piece = lax.all_gather(keys, 'blk', axis=0, tiled=True)]
    unnamed x4 -> x49, local copies, waits for them, and re-layouts: 1.26 us -> 12.1 us
    all_gather x1, blocking collectives: 23.3 us -> 18.2 us  [shards(): whole_table = lax.all_gather(group_table, 'blk', axis=0, tiled=True)]
  transfers between devices with their start and end apart: 2 -> 16, of which waited for: 2 -> 14; matrix products, arithmetic and copies ran while one was open for 3% -> 8% of each run, Pallas kernels for 0% -> 0%
where the time goes in v1:
time: 245 us; the launch traced here: 243 us
  waiting for transfers between devices  126 us (51%)
  local copies, waits for them, and re-layouts  50.3 us (21%)
  blocking collectives  18.2 us (7%)
  between operations  13.8 us (6%)
  matrix products  12.5 us (5%)
  loops' own time  11.7 us (5%)
  other arithmetic  9.24 us (4%)
    ppermute x15, waiting for transfers between devices, shards(): lax.ppermute(made[-1], 'blk', [(d, (d + 1) % nd) for d in range(nd)])  126 us
    dynamic_slice x64, local copies, waits for them, and re-layouts, shards(): lax.scan(step, initial, (key_shards, value_shards, shard_ids))  30.8 us
    all_gather x1, blocking collectives, shards(): whole_table = lax.all_gather(group_table, 'blk', axis=0, tiled=True)  18.2 us
    unnamed x49, local copies, waits for them, and re-layouts  12.1 us
    another operation x1, loops' own time, shards(): lax.scan(step, initial, (key_shards, value_shards, shard_ids))  11.7 us
    dot_general x16, matrix products, attend_shard(): jnp.einsum('hqk,khd->qhd', weights.astype(jnp.bfloat16), value_heads, pre...  6.56 us
    dot_general x16, matrix products, attend_shard(): jnp.einsum('qhd,khd->hqk', query_heads, key_heads, preferred_element_type...  5.93 us
  transfers between devices with their start and end apart: 16, of which 14 were waited for; matrix products, arithmetic and copies ran while one was open for 8% of the time, Pallas kernels for 0%

profile of v1, /device:TPU:0, one launch (start us, length us, event | category | flops | bytes accessed | tf_op | source)
XLA Modules:
  0.0 242.5 jit_solution(11480840652181795494)
XLA Ops:
  7.0 9.3 %collective-permute-done = bf16[256,512]{1,0:T(8,128)(2,1)S(1)} collective-permute-done((bf16[256,512]{1,0:T(8,128)(2,1)}, bf16[256,512]{1,0:T(8,128)(2,1)S(1)}, u32[]{:S(2)}, u32[]{:S(2)}) %collective-permute-start) | collective-permute-done | bytes 262176 | tf_op jit(solution)/shard_map/ppermute | solution.py:62
  16.3 8.5 %collective-permute-done.1 = bf16[256,512]{1,0:T(8,128)(2,1)S(1)} collective-permute-done((bf16[256,512]{1,0:T(8,128)(2,1)S(1)}, bf16[256,512]{1,0:T(8,128)(2,1)S(1)}, u32[]{:S(2)}, u32[]{:S(2)}) %collective-permute-start.1) | collective-permute-done | bytes 262176 | tf_op jit(solution)/shard_map/ppermute | solution.py:62
  24.8 8.5 %collective-permute-done.2 = bf16[256,512]{1,0:T(8,128)(2,1)S(1)} collective-permute-done((bf16[256,512]{1,0:T(8,128)(2,1)S(1)}, bf16[256,512]{1,0:T(8,128)(2,1)S(1)}, u32[]{:S(2)}, u32[]{:S(2)}) %collective-permute-start.2) | collective-permute-done | bytes 262176 | tf_op jit(solution)/shard_map/ppermute | solution.py:62
  33.3 11.7 %collective-permute-done.3 = bf16[256,512]{1,0:T(8,128)(2,1)S(1)} collective-permute-done((bf16[256,512]{1,0:T(8,128)(2,1)S(1)}, bf16[256,512]{1,0:T(8,128)(2,1)S(1)}, u32[]{:S(2)}, u32[]{:S(2)}) %collective-permute-start.3) | collective-permute-done | bytes 262176 | tf_op jit(solution)/shard_map/ppermute | solution.py:62
  45.0 8.7 %collective-permute-done.4 = bf16[256,512]{1,0:T(8,128)(2,1)S(1)} collective-permute-done((bf16[256,512]{1,0:T(8,128)(2,1)S(1)}, bf16[256,512]{1,0:T(8,128)(2,1)S(1)}, u32[]{:S(2)}, u32[]{:S(2)}) %collective-permute-start.4) | collective-permute-done | bytes 262176 | tf_op jit(solution)/shard_map/ppermute | solution.py:62
  53.7 11.9 %collective-permute-done.5 = bf16[256,512]{1,0:T(8,128)(2,1)S(1)} collective-permute-done((bf16[256,512]{1,0:T(8,128)(2,1)S(1)}, bf16[256,512]{1,0:T(8,128)(2,1)S(1)}, u32[]{:S(2)}, u32[]{:S(2)}) %collective-permute-start.5) | collective-permute-done | bytes 262176 | tf_op jit(solution)/shard_map/ppermute | solution.py:62
  65.6 13.8 %collective-permute-done.6 = bf16[256,512]{1,0:T(8,128)(2,1)S(1)} collective-permute-done((bf16[256,512]{1,0:T(8,128)(2,1)S(1)}, bf16[256,512]{1,0:T(8,128)(2,1)S(1)}, u32[]{:S(2)}, u32[]{:S(2)}) %collective-permute-start.6) | collective-permute-done | bytes 262176 | tf_op jit(solution)/shard_map/ppermute | solution.py:62
  79.5 8.5 %collective-permute-done.7 = bf16[256,512]{1,0:T(8,128)(2,1)S(1)} collective-permute-done((bf16[256,512]{1,0:T(8,128)(2,1)S(1)}, bf16[256,512]{1,0:T(8,128)(2,1)S(1)}, u32[]{:S(2)}, u32[]{:S(2)}) %collective-permute-start.7) | collective-permute-done | bytes 262176 | tf_op jit(solution)/shard_map/ppermute | solution.py:62
  88.0 8.5 %collective-permute-done.8 = bf16[256,512]{1,0:T(8,128)(2,1)S(1)} collective-permute-done((bf16[256,512]{1,0:T(8,128)(2,1)S(1)}, bf16[256,512]{1,0:T(8,128)(2,1)S(1)}, u32[]{:S(2)}, u32[]{:S(2)}) %collective-permute-start.8) | collective-permute-done | bytes 262176 | tf_op jit(solution)/shard_map/ppermute | solution.py:62
  96.4 8.5 %collective-permute-done.9 = bf16[256,512]{1,0:T(8,128)(2,1)S(1)} collective-permute-done((bf16[256,512]{1,0:T(8,128)(2,1)S(1)}, bf16[256,512]{1,0:T(8,128)(2,1)S(1)}, u32[]{:S(2)}, u32[]{:S(2)}) %collective-permute-start.9) | collective-permute-done | bytes 262176 | tf_op jit(solution)/shard_map/ppermute | solution.py:62
  104.9 8.5 %collective-permute-done.10 = bf16[256,512]{1,0:T(8,128)(2,1)S(1)} collective-permute-done((bf16[256,512]{1,0:T(8,128)(2,1)S(1)}, bf16[256,512]{1,0:T(8,128)(2,1)S(1)}, u32[]{:S(2)}, u32[]{:S(2)}) %collective-permute-start.10) | collective-permute-done | bytes 262176 | tf_op jit(solution)/shard_map/ppermute | solution.py:62
  113.4 18.2 %all-gather = s32[16,1,2]{2,1,0:T(1,128)S(1)} all-gather(s32[1,1,2]{2,1,0:T(1,128)} %bitcast.68), channel_id=1, replica_groups=mesh['blk'=16,'head'=2] {'blk'}, dimensions={0}, use_global_device_ids=true | all-gather | bytes 136 | tf_op jit(solution)/shard_map/all_gather | solution.py:15
  131.6 0.7 fusion.14
  132.9 0.7 multiply_reduce_fusion
  133.7 7.1 %collective-permute-done.12 = bf16[256,512]{1,0:T(8,128)(2,1)} collective-permute-done((bf16[256,512]{1,0:T(8,128)(2,1)S(1)}, bf16[256,512]{1,0:T(8,128)(2,1)}, u32[]{:S(2)}, u32[]{:S(2)}) %collective-permute-start.12) | collective-permute-done | bytes 262176 | tf_op jit(solution)/shard_map/ppermute | solution.py:62
  140.9 0.7 multiply_bitcast_fusion
  141.5 8.1 %collective-permute-done.13 = bf16[256,512]{1,0:T(8,128)(2,1)} collective-permute-done((bf16[256,512]{1,0:T(8,128)(2,1)}, bf16[256,512]{1,0:T(8,128)(2,1)}, u32[]{:S(2)}, u32[]{:S(2)}) %collective-permute-start.13) | collective-permute-done | bytes 262176 | tf_op jit(solution)/shard_map/ppermute | solution.py:62
  151.0 1.8 copy.23
  152.8 1.1 copy.25
  154.0 4.5 %collective-permute-done.14 = bf16[256,512]{1,0:T(8,128)(2,1)} collective-permute-done((bf16[256,512]{1,0:T(8,128)(2,1)}, bf16[256,512]{1,0:T(8,128)(2,1)}, u32[]{:S(2)}, u32[]{:S(2)}) %collective-permute-start.14) | collective-permute-done | bytes 262176 | tf_op jit(solution)/shard_map/ppermute | solution.py:62
  158.5 1.0 constant_dynamic-update-slice_fusion.31
  159.5 1.0 constant_dynamic-update-slice_fusion.30
  160.4 1.0 constant_dynamic-update-slice_fusion.29
  161.4 1.0 constant_dynamic-update-slice_fusion.28
  162.4 1.0 constant_dynamic-update-slice_fusion.27
  163.3 1.0 constant_dynamic-update-slice_fusion.26
  164.6 1.0 constant_dynamic-update-slice_fusion.15
  165.6 1.0 constant_dynamic-update-slice_fusion.14
  166.5 1.0 constant_dynamic-update-slice_fusion.13
  167.9 2.3 constant_dynamic-slice_fusion.2
  170.2 64.6 %while.15 = (s32[]{:T(128)}, f32[256,4,128]{0,2,1:T(8,128)S(1)}, f32[4,256]{1,0:T(4,128)S(1)}, f32[4,256]{1,0:T(4,128)S(1)}, s32[2,128]{1,0:T(2,128)S(1)}, /*ind...) while((s32[]{:T(128)}, f32[256,4,128]{0,2,1:T(8,128)S(1)}, ...), condition=%wide.region_3.4_spmd.clone, body=%wide.region_0.3_spmd.clone.sunk | while | flops 137173248 | bytes 7415023 | solution.py:76
  170.2 0.6 dynamic_slice.35
  171.8 1.1 constant_dynamic-slice_fusion.4
  174.2 0.6 dynamic_slice.35
  175.8 1.1 constant_dynamic-slice_fusion.4
  178.3 0.6 dynamic_slice.35
  179.9 1.1 constant_dynamic-slice_fusion.4
  182.3 0.6 dynamic_slice.35
  183.9 1.1 constant_dynamic-slice_fusion.4
  186.3 0.6 dynamic_slice.35
  187.9 1.1 constant_dynamic-slice_fusion.4
  190.4 0.6 dynamic_slice.35
  192.0 1.1 constant_dynamic-slice_fusion.4
  194.4 0.6 dynamic_slice.35
  196.0 1.1 constant_dynamic-slice_fusion.4
  198.4 0.6 dynamic_slice.35
  200.1 1.1 constant_dynamic-slice_fusion.4
  202.5 0.6 dynamic_slice.35
  204.1 1.1 constant_dynamic-slice_fusion.4
  206.5 0.6 dynamic_slice.35
  208.1 1.1 constant_dynamic-slice_fusion.4
  210.6 0.6 dynamic_slice.35
  212.2 1.1 constant_dynamic-slice_fusion.4
  214.6 0.6 dynamic_slice.35
  216.2 1.1 constant_dynamic-slice_fusion.4
  218.6 0.6 dynamic_slice.35
  220.2 1.1 constant_dynamic-slice_fusion.4
  222.7 0.6 dynamic_slice.35
  224.3 1.1 constant_dynamic-slice_fusion.4
  226.7 0.6 dynamic_slice.35
  228.3 1.1 constant_dynamic-slice_fusion.4
  230.7 0.6 dynamic_slice.35
  232.4 1.1 constant_dynamic-slice_fusion.4
  234.8 0.8 copy.30
  (264 shorter events, 29.5 us)
Async XLA Ops:
  6.5 143.3 %copy-start = (s32[4096]{0:T(1024)S(1)}, s32[4096]{0:T(1024)}, u32[]{:S(2)}) copy-start(s32[4096]{0:T(1024)} %param.11) | copy-start | bytes 49156
  6.5 158.0 %copy-start.1 = (bf16[256,512]{1,0:T(8,128)(2,1)S(1)}, bf16[256,512]{1,0:T(8,128)(2,1)}, u32[]{:S(2)}) copy-start(bf16[256,512]{1,0:T(8,128)(2,1)} %param.9) | copy-start | bytes 786436
  6.5 163.6 %all-gather.3.cloned.1.call-start = ((), (), s32[]{:S(2)}) async-start(), calls=%async_computation | async-start | bytes 4456448 | tf_op jit(solution)/shard_map/all_gather | solution.py:58
  6.5 9.8 %collective-permute-start = (bf16[256,512]{1,0:T(8,128)(2,1)}, bf16[256,512]{1,0:T(8,128)(2,1)S(1)}, u32[]{:S(2)}, u32[]{:S(2)}) collective-permute-start(bf16[256,512]{1,0:T(8,128)(2,1)} %param.9), channel_id=1, source_target_pairs={{0,2},{2,4},{4,6},{6,8},{8,10},{10,12},{12,14},{14,16},{16,18},{18... | collective-permute-start | bytes 786440 | tf_op jit(solution)/shard_map/ppermute | solution.py:62
  16.3 8.5 %collective-permute-start.1 = (bf16[256,512]{1,0:T(8,128)(2,1)S(1)}, bf16[256,512]{1,0:T(8,128)(2,1)S(1)}, u32[]{:S(2)}, u32[]{:S(2)}) collective-permute-start(bf16[256,512]{1,0:T(8,128)(2,1)S(1)} %collective-permute-done), channel_id=1, source_target_pairs={{0,2},{2,4},{4,6},{6,8},{8,10},{10,12},{12,14},{14,16},{16,18},{18... | collective-permute-start | bytes 786440 | tf_op jit(solution)/shard_map/ppermute | solution.py:62
  24.8 8.5 %collective-permute-start.2 = (bf16[256,512]{1,0:T(8,128)(2,1)S(1)}, bf16[256,512]{1,0:T(8,128)(2,1)S(1)}, u32[]{:S(2)}, u32[]{:S(2)}) collective-permute-start(bf16[256,512]{1,0:T(8,128)(2,1)S(1)} %collective-permute-done.1), channel_id=1, source_target_pairs={{0,2},{2,4},{4,6},{6,8},{8,10},{10,12},{12,14},{14,16},{16,18},{18... | collective-permute-start | bytes 786440 | tf_op jit(solution)/shard_map/ppermute | solution.py:62
  33.3 11.7 %collective-permute-start.3 = (bf16[256,512]{1,0:T(8,128)(2,1)S(1)}, bf16[256,512]{1,0:T(8,128)(2,1)S(1)}, u32[]{:S(2)}, u32[]{:S(2)}) collective-permute-start(bf16[256,512]{1,0:T(8,128)(2,1)S(1)} %collective-permute-done.2), channel_id=1, source_target_pairs={{0,2},{2,4},{4,6},{6,8},{8,10},{10,12},{12,14},{14,16},{16,18},{18... | collective-permute-start | bytes 786440 | tf_op jit(solution)/shard_map/ppermute | solution.py:62
  45.0 8.7 %collective-permute-start.4 = (bf16[256,512]{1,0:T(8,128)(2,1)S(1)}, bf16[256,512]{1,0:T(8,128)(2,1)S(1)}, u32[]{:S(2)}, u32[]{:S(2)}) collective-permute-start(bf16[256,512]{1,0:T(8,128)(2,1)S(1)} %collective-permute-done.3), channel_id=1, source_target_pairs={{0,2},{2,4},{4,6},{6,8},{8,10},{10,12},{12,14},{14,16},{16,18},{18... | collective-permute-start | bytes 786440 | tf_op jit(solution)/shard_map/ppermute | solution.py:62
  53.7 11.9 %collective-permute-start.5 = (bf16[256,512]{1,0:T(8,128)(2,1)S(1)}, bf16[256,512]{1,0:T(8,128)(2,1)S(1)}, u32[]{:S(2)}, u32[]{:S(2)}) collective-permute-start(bf16[256,512]{1,0:T(8,128)(2,1)S(1)} %collective-permute-done.4), channel_id=1, source_target_pairs={{0,2},{2,4},{4,6},{6,8},{8,10},{10,12},{12,14},{14,16},{16,18},{18... | collective-permute-start | bytes 786440 | tf_op jit(solution)/shard_map/ppermute | solution.py:62
  65.6 13.8 %collective-permute-start.6 = (bf16[256,512]{1,0:T(8,128)(2,1)S(1)}, bf16[256,512]{1,0:T(8,128)(2,1)S(1)}, u32[]{:S(2)}, u32[]{:S(2)}) collective-permute-start(bf16[256,512]{1,0:T(8,128)(2,1)S(1)} %collective-permute-done.5), channel_id=1, source_target_pairs={{0,2},{2,4},{4,6},{6,8},{8,10},{10,12},{12,14},{14,16},{16,18},{18... | collective-permute-start | bytes 786440 | tf_op jit(solution)/shard_map/ppermute | solution.py:62
  79.5 8.5 %collective-permute-start.7 = (bf16[256,512]{1,0:T(8,128)(2,1)S(1)}, bf16[256,512]{1,0:T(8,128)(2,1)S(1)}, u32[]{:S(2)}, u32[]{:S(2)}) collective-permute-start(bf16[256,512]{1,0:T(8,128)(2,1)S(1)} %collective-permute-done.6), channel_id=1, source_target_pairs={{0,2},{2,4},{4,6},{6,8},{8,10},{10,12},{12,14},{14,16},{16,18},{18... | collective-permute-start | bytes 786440 | tf_op jit(solution)/shard_map/ppermute | solution.py:62
  87.9 8.5 %collective-permute-start.8 = (bf16[256,512]{1,0:T(8,128)(2,1)S(1)}, bf16[256,512]{1,0:T(8,128)(2,1)S(1)}, u32[]{:S(2)}, u32[]{:S(2)}) collective-permute-start(bf16[256,512]{1,0:T(8,128)(2,1)S(1)} %collective-permute-done.7), channel_id=1, source_target_pairs={{0,2},{2,4},{4,6},{6,8},{8,10},{10,12},{12,14},{14,16},{16,18},{18... | collective-permute-start | bytes 786440 | tf_op jit(solution)/shard_map/ppermute | solution.py:62
  96.4 8.5 %collective-permute-start.9 = (bf16[256,512]{1,0:T(8,128)(2,1)S(1)}, bf16[256,512]{1,0:T(8,128)(2,1)S(1)}, u32[]{:S(2)}, u32[]{:S(2)}) collective-permute-start(bf16[256,512]{1,0:T(8,128)(2,1)S(1)} %collective-permute-done.8), channel_id=1, source_target_pairs={{0,2},{2,4},{4,6},{6,8},{8,10},{10,12},{12,14},{14,16},{16,18},{18... | collective-permute-start | bytes 786440 | tf_op jit(solution)/shard_map/ppermute | solution.py:62
  104.9 44.8 %copy-start.2 = (bf16[256,512]{1,0:T(8,128)(2,1)}, bf16[256,512]{1,0:T(8,128)(2,1)S(1)}, u32[]{:S(2)}) copy-start(bf16[256,512]{1,0:T(8,128)(2,1)S(1)} %collective-permute-done.9) | copy-start | bytes 786436
  104.9 8.5 %collective-permute-start.10 = (bf16[256,512]{1,0:T(8,128)(2,1)S(1)}, bf16[256,512]{1,0:T(8,128)(2,1)S(1)}, u32[]{:S(2)}, u32[]{:S(2)}) collective-permute-start(bf16[256,512]{1,0:T(8,128)(2,1)S(1)} %collective-permute-done.9), channel_id=1, source_target_pairs={{0,2},{2,4},{4,6},{6,8},{8,10},{10,12},{12,14},{14,16},{16,18},{18... | collective-permute-start | bytes 786440 | tf_op jit(solution)/shard_map/ppermute | solution.py:62
  113.4 36.3 %copy-start.4 = (bf16[256,512]{1,0:T(8,128)(2,1)}, bf16[256,512]{1,0:T(8,128)(2,1)S(1)}, u32[]{:S(2)}) copy-start(bf16[256,512]{1,0:T(8,128)(2,1)S(1)} %collective-permute-done.10) | copy-start | bytes 786436
  113.4 18.8 %collective-permute-start.11 = (bf16[256,512]{1,0:T(8,128)(2,1)S(1)}, bf16[256,512]{1,0:T(8,128)(2,1)S(1)}, u32[]{:S(2)}, u32[]{:S(2)}) collective-permute-start(bf16[256,512]{1,0:T(8,128)(2,1)S(1)} %collective-permute-done.10), channel_id=1, source_target_pairs={{0,2},{2,4},{4,6},{6,8},{8,10},{10,12},{12,14},{14,16},{16,18},{18... | collective-permute-start | bytes 786440 | tf_op jit(solution)/shard_map/ppermute | solution.py:62
  132.3 17.5 %copy-start.6 = (bf16[256,512]{1,0:T(8,128)(2,1)}, bf16[256,512]{1,0:T(8,128)(2,1)S(1)}, u32[]{:S(2)}) copy-start(bf16[256,512]{1,0:T(8,128)(2,1)S(1)} %collective-permute-done.11) | copy-start | bytes 786436
  132.3 8.6 %collective-permute-start.12 = (bf16[256,512]{1,0:T(8,128)(2,1)S(1)}, bf16[256,512]{1,0:T(8,128)(2,1)}, u32[]{:S(2)}, u32[]{:S(2)}) collective-permute-start(bf16[256,512]{1,0:T(8,128)(2,1)S(1)} %collective-permute-done.11), channel_id=1, source_target_pairs={{0,2},{2,4},{4,6},{6,8},{8,10},{10,12},{12,14},{14,16},{16,18},{18... | collective-permute-start | bytes 786440 | tf_op jit(solution)/shard_map/ppermute | solution.py:62
  140.9 8.8 %collective-permute-start.13 = (bf16[256,512]{1,0:T(8,128)(2,1)}, bf16[256,512]{1,0:T(8,128)(2,1)}, u32[]{:S(2)}, u32[]{:S(2)}) collective-permute-start(bf16[256,512]{1,0:T(8,128)(2,1)} %collective-permute-done.12), channel_id=1, source_target_pairs={{0,2},{2,4},{4,6},{6,8},{8,10},{10,12},{12,14},{14,16},{16,18},{18... | collective-permute-start | bytes 786440 | tf_op jit(solution)/shard_map/ppermute | solution.py:62
  149.7 8.8 %collective-permute-start.14 = (bf16[256,512]{1,0:T(8,128)(2,1)}, bf16[256,512]{1,0:T(8,128)(2,1)}, u32[]{:S(2)}, u32[]{:S(2)}) collective-permute-start(bf16[256,512]{1,0:T(8,128)(2,1)} %collective-permute-done.13), channel_id=1, source_target_pairs={{0,2},{2,4},{4,6},{6,8},{8,10},{10,12},{12,14},{14,16},{16,18},{18... | collective-permute-start | bytes 786440 | tf_op jit(solution)/shard_map/ppermute | solution.py:62
  153.9 13.6 %copy-start.7 = (bf16[256,512]{1,0:T(8,128)(2,1)S(1)}, bf16[256,512]{1,0:T(8,128)(2,1)}, u32[]{:S(2)}) copy-start(bf16[256,512]{1,0:T(8,128)(2,1)} %copy-done.6) | copy-start | bytes 786436
  153.9 13.6 %copy-start.5 = (bf16[256,512]{1,0:T(8,128)(2,1)S(1)}, bf16[256,512]{1,0:T(8,128)(2,1)}, u32[]{:S(2)}) copy-start(bf16[256,512]{1,0:T(8,128)(2,1)} %copy-done.4) | copy-start | bytes 786436
  153.9 13.7 %copy-start.3 = (bf16[256,512]{1,0:T(8,128)(2,1)S(1)}, bf16[256,512]{1,0:T(8,128)(2,1)}, u32[]{:S(2)}) copy-start(bf16[256,512]{1,0:T(8,128)(2,1)} %copy-done.2) | copy-start | bytes 786436
Sparse Core Ops, SparseCore 0:
  25.0 56.9 all-gather.2
